TPU v7x, 128 devices: a whole 4x4x4 slice. The times are simulated.
128 devices in a mesh: depth: 8 (over x, z_hi), screen: 16 (over z_lo, y, core).
Axes of the slice: x: 4, y: 4, z: 4 (z_hi: 2, z_lo: 2; z = z_hi * 2 + z_lo), core: 2. Of those that a mesh axis runs over, the one named last changes fastest.
Arguments:
- voxel_bins: int32 [64, 256, 4096], P('depth', None, 'screen'), may hold values from 0 to 255
- colors: bfloat16 [3, 256], replicated, may hold values from 0 to 2
- opacity: bfloat16 [256], replicated, may hold values from 0 to 1
- slab_order: int32 [16, 8], replicated, may hold values from 0 to 7, each once within a row
Outputs:
- image: float32 [4, 256, 4096], P(None, ('depth', 'screen'))
Inputs may be any that keep to these rules, and one draw needn't show every extreme that they name: `slab_order`: every row is a permutation of 0 to 7.
All inputs are finite; a program needn't handle non-finite values.
Results may differ from a plain program's by a relative error of at most 0.0003.
Values sent between devices are 32-bit elements; how exact they have to be, the bound alone decides.
A program may use at most 64 MiB of HBM per device.

v0:
```python
import math
import jax
import jax.numpy as jnp
from jax import lax
from jax.sharding import PartitionSpec as P

low_count = 16
extinction = 3.0


def look_up(table_rows, bin_block):
    high_count = table_rows.shape[0] // 4
    low_part = bin_block % low_count
    high_part = bin_block // low_count
    low_onehot = (low_part[None, :] == jnp.arange(low_count, dtype=jnp.int32)[:, None]).astype(
        jnp.bfloat16
    )
    picked = jnp.dot(table_rows, low_onehot, preferred_element_type=jnp.float32)
    picked = picked.reshape(4, high_count, bin_block.shape[0])
    high_match = high_part[None, :] == jnp.arange(high_count, dtype=jnp.int32)[:, None]
    return jnp.sum(jnp.where(high_match[None], picked, 0.0), axis=1)


def render(voxel_bins, table_rows, total_samples):
    samples_here, row_count, col_count = voxel_bins.shape
    pixels = row_count * col_count
    per_step = math.gcd(samples_here, max(1, 131072 // pixels))
    blocks = voxel_bins.reshape(samples_here // per_step, per_step * pixels)
    extinct_rate = extinction / total_samples

    def advance(carried, bin_block):
        passed, color_sum = carried
        values = look_up(table_rows, bin_block).reshape(4, per_step, pixels)
        density = values[3]
        before = jnp.cumsum(density, axis=0) - density
        weight = (1.0 - jnp.exp(-extinct_rate * density)) * jnp.exp(
            -extinct_rate * (passed[None] + before)
        )
        color_sum = color_sum + jnp.sum(weight[None] * values[:3], axis=1)
        return ((passed + jnp.sum(density, axis=0), color_sum), None)

    start = (jnp.zeros((pixels,), jnp.float32), jnp.zeros((3, pixels), jnp.float32))
    (passed, color_sum), ignored = lax.scan(advance, start, blocks)
    final_alpha = 1.0 - jnp.exp(-extinct_rate * passed)
    partial_value = jnp.concatenate([color_sum, final_alpha[None]], axis=0)
    return partial_value.reshape(4, row_count, col_count)


def composite(pieces, places):
    in_front = (places[:, None, :] < places[:, :, None]).astype(jnp.float32)
    clear_log = jnp.log1p(-pieces[:, :, 3])
    front_log = jnp.einsum("tij,jtrw->itrw", in_front, clear_log, precision=lax.Precision.HIGHEST)
    shaded = jnp.sum(pieces[:, :, :3] * jnp.exp(front_log)[:, :, None], axis=0)
    total_alpha = 1.0 - jnp.exp(jnp.sum(clear_log, axis=0))
    merged = jnp.concatenate([shaded, total_alpha[:, None]], axis=1)
    return jnp.transpose(merged, (1, 2, 0, 3))


def local(voxel_bins, colors, opacity, slab_order):
    table = jnp.concatenate([colors, opacity[None]], axis=0)
    table_rows = table.reshape(4 * (table.shape[1] // low_count), low_count)
    depth_count = lax.axis_size("depth")
    screen_count = lax.axis_size("screen")
    total_samples = voxel_bins.shape[0] * depth_count
    partial_value = render(voxel_bins, table_rows, total_samples)
    row_count = partial_value.shape[1]
    col_count = partial_value.shape[2]
    owned_rows = row_count // (depth_count * screen_count)
    pieces = lax.all_to_all(
        partial_value[None], ("depth", "screen"), split_axis=2, concat_axis=0, tiled=True
    )
    ordered = pieces.reshape(depth_count, screen_count, 4, pieces.shape[2], pieces.shape[3])
    joined = composite(ordered, slab_order)
    result = joined.reshape(4, owned_rows, screen_count * col_count)
    return result


def solution(mesh):
    placed = (P("depth", None, "screen"), P(), P(), P())
    return jax.shard_map(
        local,
        mesh=mesh,
        in_specs=placed,
        out_specs=P(None, ("depth", "screen"), None),
        check_vma=False,
    )
```

profile of v0, /device:TPU:1, one launch (start us, length us, event | category | flops | bytes accessed | tf_op | source)
XLA Modules:
  0.0 180.9 jit_solution(15716639711246271932)
XLA Ops:
  0.0 4.0 %reshape.117 = s32[4,131072]{1,0:T(4,128)} reshape(s32[8,256,256]{2,1,0:T(8,128)} %param.6) | data formatting | bytes 4194304 | tf_op jit(solution)/shard_map/reshape | solution.py:28
  4.2 140.2 %while.15 = (s32[]{:T(128)}, f32[65536]{0:T(1024)}, f32[3,65536]{1,0:T(4,128)}, s32[4,131072]{1,0:T(4,128)}, bf16[64,16]{0,1:T(8,128)(2,1)S(1)}, /*index=5*/s32[]{:T(128)}, f32[]{:T(128)}, s32[]{:T(128)}) while((s32[]{:T(128)}, f32[65536]{0:T(1024)}, f32[3,65536]{1,0:T(4,128)}, s32[4,131072]{1,0:T(4,128)}, ...), condition=%wide.region_5.6_spmd.clone, body=%wide.region_0.5_spmd.clone.sunk | while | flops 293994496 | bytes 31983784 | solution.py:43
  4.2 3.4 %and_select_fusion.4 = (s32[1,131072]{1,0:T(1,128)S(1)}, s32[1,131072]{1,0:T(1,128)S(1)}) fusion(s32[4,131072]{1,0:T(4,128)} %get-tuple-element.186, s32[]{:T(128)} %get-tuple-element.175), kind=kLoop, calls=%fused_computation.5.clone.1 | loop fusion | flops 1441792 | bytes 1572868 | tf_op jit(solution)/shard_map/while/body/eval_jaxpr/jit(remainder)/select_n | solution.py:13
  7.6 3.8 %and_select_fusion.5 = s32[1,131072]{1,0:T(1,128)S(1)} fusion(s32[1,131072]{1,0:T(1,128)S(1)} %get-tuple-element.163, s32[4,131072]{1,0:T(4,128)} %get-tuple-element.186, s32[]{:T(128)} %get-tuple-element.175), kind=kLoop, calls=%fused_computation.6.clone.1 | loop fusion | flops 1572864 | bytes 1572868 | tf_op jit(solution)/shard_map/while/body/eval_jaxpr/jit(floor_divide)/jit(_where)/select_n | solution.py:14
  12.5 11.0 %select_reduce_fusion.2 = f32[4,131072]{1,0:T(4,128)S(1)} fusion(pred[16,131072]{1,0:T(8,128)(4,1)S(1)} %iota_compare_fusion.4, bf16[64,16]{0,1:T(8,128)(2,1)S(1)} %get-tuple-element.187, s32[131072]{0:T(1024)S(1)} %bitcast.42), kind=kOutput, calls=%fused_computation.clone.1 | convolution fusion | flops 286785536 | bytes 4720640 | tf_op jit(solution)/shard_map/while/body/eval_jaxpr/dot_general | solution.py:18
  30.3 2.9 %slice.38 = f32[3,2,65536]{2,1,0:T(2,128)} reshape(f32[3,131072]{1,0:T(4,128)S(1)} %bitcast.40) | data formatting | bytes 3145728 | tf_op jit(solution)/shard_map/while/body/eval_jaxpr/slice | solution.py:39
  33.1 3.9 %multiply_reduce_fusion.2 = f32[3,65536]{1,0:T(4,128)S(1)} fusion(f32[3,2,65536]{2,1,0:T(2,128)} %slice.38, f32[2,65536]{1,0:T(2,128)S(1)} %exponential_multiply_fusion.2), kind=kLoop, calls=%fused_computation.7.clone.1 | loop fusion | flops 589824 | bytes 2883584 | tf_op jit(solution)/shard_map/while/body/eval_jaxpr/reduce_sum | solution.py:39
  38.6 3.4 %and_select_fusion.4 = (s32[1,131072]{1,0:T(1,128)S(1)}, s32[1,131072]{1,0:T(1,128)S(1)}) fusion(s32[4,131072]{1,0:T(4,128)} %get-tuple-element.186, s32[]{:T(128)} %get-tuple-element.175), kind=kLoop, calls=%fused_computation.5.clone.1 | loop fusion | flops 1441792 | bytes 1572868 | tf_op jit(solution)/shard_map/while/body/eval_jaxpr/jit(remainder)/select_n | solution.py:13
  41.9 3.8 %and_select_fusion.5 = s32[1,131072]{1,0:T(1,128)S(1)} fusion(s32[1,131072]{1,0:T(1,128)S(1)} %get-tuple-element.163, s32[4,131072]{1,0:T(4,128)} %get-tuple-element.186, s32[]{:T(128)} %get-tuple-element.175), kind=kLoop, calls=%fused_computation.6.clone.1 | loop fusion | flops 1572864 | bytes 1572868 | tf_op jit(solution)/shard_map/while/body/eval_jaxpr/jit(floor_divide)/jit(_where)/select_n | solution.py:14
  46.8 11.0 %select_reduce_fusion.2 = f32[4,131072]{1,0:T(4,128)S(1)} fusion(pred[16,131072]{1,0:T(8,128)(4,1)S(1)} %iota_compare_fusion.4, bf16[64,16]{0,1:T(8,128)(2,1)S(1)} %get-tuple-element.187, s32[131072]{0:T(1024)S(1)} %bitcast.42), kind=kOutput, calls=%fused_computation.clone.1 | convolution fusion | flops 286785536 | bytes 4720640 | tf_op jit(solution)/shard_map/while/body/eval_jaxpr/dot_general | solution.py:18
  65.6 2.9 %slice.38 = f32[3,2,65536]{2,1,0:T(2,128)} reshape(f32[3,131072]{1,0:T(4,128)S(1)} %bitcast.40) | data formatting | bytes 3145728 | tf_op jit(solution)/shard_map/while/body/eval_jaxpr/slice | solution.py:39
  68.4 3.9 %multiply_reduce_fusion.2 = f32[3,65536]{1,0:T(4,128)S(1)} fusion(f32[3,2,65536]{2,1,0:T(2,128)} %slice.38, f32[2,65536]{1,0:T(2,128)S(1)} %exponential_multiply_fusion.2), kind=kLoop, calls=%fused_computation.7.clone.1 | loop fusion | flops 589824 | bytes 2883584 | tf_op jit(solution)/shard_map/while/body/eval_jaxpr/reduce_sum | solution.py:39
  73.9 3.4 %and_select_fusion.4 = (s32[1,131072]{1,0:T(1,128)S(1)}, s32[1,131072]{1,0:T(1,128)S(1)}) fusion(s32[4,131072]{1,0:T(4,128)} %get-tuple-element.186, s32[]{:T(128)} %get-tuple-element.175), kind=kLoop, calls=%fused_computation.5.clone.1 | loop fusion | flops 1441792 | bytes 1572868 | tf_op jit(solution)/shard_map/while/body/eval_jaxpr/jit(remainder)/select_n | solution.py:13
  77.2 3.8 %and_select_fusion.5 = s32[1,131072]{1,0:T(1,128)S(1)} fusion(s32[1,131072]{1,0:T(1,128)S(1)} %get-tuple-element.163, s32[4,131072]{1,0:T(4,128)} %get-tuple-element.186, s32[]{:T(128)} %get-tuple-element.175), kind=kLoop, calls=%fused_computation.6.clone.1 | loop fusion | flops 1572864 | bytes 1572868 | tf_op jit(solution)/shard_map/while/body/eval_jaxpr/jit(floor_divide)/jit(_where)/select_n | solution.py:14
  82.1 11.0 %select_reduce_fusion.2 = f32[4,131072]{1,0:T(4,128)S(1)} fusion(pred[16,131072]{1,0:T(8,128)(4,1)S(1)} %iota_compare_fusion.4, bf16[64,16]{0,1:T(8,128)(2,1)S(1)} %get-tuple-element.187, s32[131072]{0:T(1024)S(1)} %bitcast.42), kind=kOutput, calls=%fused_computation.clone.1 | convolution fusion | flops 286785536 | bytes 4720640 | tf_op jit(solution)/shard_map/while/body/eval_jaxpr/dot_general | solution.py:18
  100.8 2.9 %slice.38 = f32[3,2,65536]{2,1,0:T(2,128)} reshape(f32[3,131072]{1,0:T(4,128)S(1)} %bitcast.40) | data formatting | bytes 3145728 | tf_op jit(solution)/shard_map/while/body/eval_jaxpr/slice | solution.py:39
  103.7 3.9 %multiply_reduce_fusion.2 = f32[3,65536]{1,0:T(4,128)S(1)} fusion(f32[3,2,65536]{2,1,0:T(2,128)} %slice.38, f32[2,65536]{1,0:T(2,128)S(1)} %exponential_multiply_fusion.2), kind=kLoop, calls=%fused_computation.7.clone.1 | loop fusion | flops 589824 | bytes 2883584 | tf_op jit(solution)/shard_map/while/body/eval_jaxpr/reduce_sum | solution.py:39
  109.1 3.4 %and_select_fusion.4 = (s32[1,131072]{1,0:T(1,128)S(1)}, s32[1,131072]{1,0:T(1,128)S(1)}) fusion(s32[4,131072]{1,0:T(4,128)} %get-tuple-element.186, s32[]{:T(128)} %get-tuple-element.175), kind=kLoop, calls=%fused_computation.5.clone.1 | loop fusion | flops 1441792 | bytes 1572868 | tf_op jit(solution)/shard_map/while/body/eval_jaxpr/jit(remainder)/select_n | solution.py:13
  112.5 3.8 %and_select_fusion.5 = s32[1,131072]{1,0:T(1,128)S(1)} fusion(s32[1,131072]{1,0:T(1,128)S(1)} %get-tuple-element.163, s32[4,131072]{1,0:T(4,128)} %get-tuple-element.186, s32[]{:T(128)} %get-tuple-element.175), kind=kLoop, calls=%fused_computation.6.clone.1 | loop fusion | flops 1572864 | bytes 1572868 | tf_op jit(solution)/shard_map/while/body/eval_jaxpr/jit(floor_divide)/jit(_where)/select_n | solution.py:14
  117.4 11.0 %select_reduce_fusion.2 = f32[4,131072]{1,0:T(4,128)S(1)} fusion(pred[16,131072]{1,0:T(8,128)(4,1)S(1)} %iota_compare_fusion.4, bf16[64,16]{0,1:T(8,128)(2,1)S(1)} %get-tuple-element.187, s32[131072]{0:T(1024)S(1)} %bitcast.42), kind=kOutput, calls=%fused_computation.clone.1 | convolution fusion | flops 286785536 | bytes 4720640 | tf_op jit(solution)/shard_map/while/body/eval_jaxpr/dot_general | solution.py:18
  136.1 2.9 %slice.38 = f32[3,2,65536]{2,1,0:T(2,128)} reshape(f32[3,131072]{1,0:T(4,128)S(1)} %bitcast.40) | data formatting | bytes 3145728 | tf_op jit(solution)/shard_map/while/body/eval_jaxpr/slice | solution.py:39
  139.0 3.9 %multiply_reduce_fusion.2 = f32[3,65536]{1,0:T(4,128)S(1)} fusion(f32[3,2,65536]{2,1,0:T(2,128)} %slice.38, f32[2,65536]{1,0:T(2,128)S(1)} %exponential_multiply_fusion.2), kind=kLoop, calls=%fused_computation.7.clone.1 | loop fusion | flops 589824 | bytes 2883584 | tf_op jit(solution)/shard_map/while/body/eval_jaxpr/reduce_sum | solution.py:39
  148.1 11.5 %all-to-all-start = ((f32[1,4,256,256]{3,1,0,2:T(4,128)}), f32[1,4,256,256]{3,1,0,2:T(4,128)S(1)}, u32[]{:S(2)}, u32[]{:S(2)}) async-start(f32[1,4,256,256]{3,1,0,2:T(4,128)} %pad_maximum_fusion), calls=%async_computation | async-start | bytes 2097152 | tf_op jit(solution)/shard_map/all_to_all | solution.py:69
  159.7 18.9 %all-to-all-done = f32[1,4,256,256]{3,1,0,2:T(4,128)S(1)} async-done(((f32[1,4,256,256]{3,1,0,2:T(4,128)}), f32[1,4,256,256]{3,1,0,2:T(4,128)S(1)}, u32[]{:S(2)}, u32[]{:S(2)}) %all-to-all-start) | async-done | bytes 1048608 | tf_op jit(solution)/shard_map/all_to_all | solution.py:69
  (73 shorter events, 46.8 us)
Async XLA Ops:
  0.0 4.0 %copy-start.4 = (bf16[256]{0:T(256)(128)(2,1)S(1)}, bf16[256]{0:T(256)(128)(2,1)}, u32[]{:S(2)}) copy-start(bf16[256]{0:T(256)(128)(2,1)} %param.8) | copy-start | bytes 1540
  0.0 4.0 %copy-start.3 = (bf16[3,256]{1,0:T(4,128)(2,1)S(1)}, bf16[3,256]{1,0:T(4,128)(2,1)}, u32[]{:S(2)}) copy-start(bf16[3,256]{1,0:T(4,128)(2,1)} %param.7) | copy-start | bytes 4612
  33.1 3.9 %copy-start = (f32[3,65536]{1,0:T(4,128)S(1)}, f32[3,65536]{1,0:T(4,128)}, u32[]{:S(2)}) copy-start(f32[3,65536]{1,0:T(4,128)} %get-tuple-element.177) | copy-start | bytes 2359300 | tf_op jit(solution)/shard_map/while
  37.6 1.0 copy-start.1
  68.4 3.9 %copy-start = (f32[3,65536]{1,0:T(4,128)S(1)}, f32[3,65536]{1,0:T(4,128)}, u32[]{:S(2)}) copy-start(f32[3,65536]{1,0:T(4,128)} %get-tuple-element.177) | copy-start | bytes 2359300 | tf_op jit(solution)/shard_map/while
  72.9 1.0 copy-start.1
  103.7 3.9 %copy-start = (f32[3,65536]{1,0:T(4,128)S(1)}, f32[3,65536]{1,0:T(4,128)}, u32[]{:S(2)}) copy-start(f32[3,65536]{1,0:T(4,128)} %get-tuple-element.177) | copy-start | bytes 2359300 | tf_op jit(solution)/shard_map/while
  108.2 1.0 copy-start.1
  139.0 3.9 %copy-start = (f32[3,65536]{1,0:T(4,128)S(1)}, f32[3,65536]{1,0:T(4,128)}, u32[]{:S(2)}) copy-start(f32[3,65536]{1,0:T(4,128)} %get-tuple-element.177) | copy-start | bytes 2359300 | tf_op jit(solution)/shard_map/while
  143.5 1.0 copy-start.1
  145.4 14.2 %copy-start.2 = (s32[16,8]{0,1:T(8,128)S(1)}, s32[16,8]{0,1:T(8,128)}, u32[]{:S(2)}) copy-start(s32[16,8]{0,1:T(8,128)} %param.9) | copy-start | bytes 1540
  148.1 30.5 %all-to-all-start = ((f32[1,4,256,256]{3,1,0,2:T(4,128)}), f32[1,4,256,256]{3,1,0,2:T(4,128)S(1)}, u32[]{:S(2)}, u32[]{:S(2)}) async-start(f32[1,4,256,256]{3,1,0,2:T(4,128)} %pad_maximum_fusion), calls=%async_computation | async-start | bytes 2097152 | tf_op jit(solution)/shard_map/all_to_all | solution.py:69
where the time goes:
time: 182 us; the launch traced here: 181 us
  other arithmetic  77.5 us (43%)
  matrix products  44.4 us (24%)
  local copies, waits for them, and re-layouts  28.1 us (15%)
  waiting for transfers between devices  18.9 us (10%)
  starting transfers between devices  11.5 us (6%)
    dot_general x4, matrix products, look_up(): picked = jnp.dot(table_rows, low_onehot, preferred_element_type=jnp.float32)  44 us
    all_to_all x1, waiting for transfers between devices, local(): lax.all_to_all(partial_value[None], ('depth', 'screen'), split_axis=2, co...  18.9 us
    reduce_sum x4, other arithmetic, advance(): color_sum = color_sum + jnp.sum(weight[None] * values[:3], axis=1)  15.4 us
    select_n x4, other arithmetic, look_up(): high_part = bin_block // low_count  15 us
    select_n x4, other arithmetic, look_up(): low_part = bin_block % low_count  13.5 us
    all_to_all x1, starting transfers between devices, local(): lax.all_to_all(partial_value[None], ('depth', 'screen'), split_axis=2, co...  11.5 us
    slice x4, local copies, waits for them, and re-layouts, advance(): color_sum = color_sum + jnp.sum(weight[None] * values[:3], axis=1)  11.4 us
    another operation x4, other arithmetic, advance(): before = jnp.cumsum(density, axis=0) - density  7.29 us
  transfers between devices with their start and end apart: 1, of which 1 were waited for; matrix products, arithmetic and copies ran while one was open for 0% of the time, Pallas kernels for 0%

commit v1 on v0

--- a/solution.py
+++ b/solution.py
@@ -66,8 +66,14 @@
     row_count = partial_value.shape[1]
     col_count = partial_value.shape[2]
     owned_rows = row_count // (depth_count * screen_count)
-    pieces = lax.all_to_all(
-        partial_value[None], ("depth", "screen"), split_axis=2, concat_axis=0, tiled=True
+    pieces = jnp.concatenate(
+        lax.all_to_all(
+            jnp.stack(jnp.split(partial_value[None], lax.axis_size(("depth", "screen")), axis=2)),
+            ("depth", "screen"),
+            0,
+            0,
+        ),
+        axis=0,
     )
     ordered = pieces.reshape(depth_count, screen_count, 4, pieces.shape[2], pieces.shape[3])
     joined = composite(ordered, slab_order)

time: 182 us -> 257 us (1.41)
  local copies, waits for them, and re-layouts: 28.1 us -> 106 us
  other arithmetic: 77.5 us -> 74.8 us
    unnamed x8 -> x136, local copies, waits for them, and re-layouts: 0.16 us -> 77.4 us
    concatenate x1 -> x0, other arithmetic: 2.72 us -> none  [render(): partial_value = jnp.concatenate([color_sum, final_alpha[None]], axis=0)]
where the time goes in v1:
time: 257 us; the launch traced here: 256 us
  local copies, waits for them, and re-layouts  106 us (41%)
  other arithmetic  74.8 us (29%)
  matrix products  44.5 us (17%)
  waiting for transfers between devices  18.9 us (7%)
  starting transfers between devices  11.5 us (4%)
    unnamed x136, local copies, waits for them, and re-layouts  77.4 us
    dot_general x4, matrix products, look_up(): picked = jnp.dot(table_rows, low_onehot, preferred_element_type=jnp.float32)  44 us
    all_to_all x1, waiting for transfers between devices, local(): lax.all_to_all(jnp.stack(jnp.split(partial_value[None], lax.axis_size(('d...  18.9 us
    reduce_sum x4, other arithmetic, advance(): color_sum = color_sum + jnp.sum(weight[None] * values[:3], axis=1)  15.4 us
    select_n x4, other arithmetic, look_up(): high_part = bin_block // low_count  15 us
    select_n x4, other arithmetic, look_up(): low_part = bin_block % low_count  13.5 us
    all_to_all x1, starting transfers between devices, local(): lax.all_to_all(jnp.stack(jnp.split(partial_value[None], lax.axis_size(('d...  11.5 us
    slice x4, local copies, waits for them, and re-layouts, advance(): color_sum = color_sum + jnp.sum(weight[None] * values[:3], axis=1)  11.4 us
  transfers between devices with their start and end apart: 1, of which 1 were waited for; matrix products, arithmetic and copies ran while one was open for 0% of the time, Pallas kernels for 0%

profile of v1, /device:TPU:1, one launch (start us, length us, event | category | flops | bytes accessed | tf_op | source)
XLA Modules:
  0.0 256.2 jit_solution(15444917599498797046)
XLA Ops:
  0.0 4.0 %reshape.113 = s32[4,131072]{1,0:T(4,128)} reshape(s32[8,256,256]{2,1,0:T(8,128)} %param.6) | data formatting | bytes 4194304 | tf_op jit(solution)/shard_map/reshape | solution.py:28
  4.2 140.2 %while.15 = (s32[]{:T(128)}, f32[65536]{0:T(1024)}, f32[3,65536]{1,0:T(4,128)}, s32[4,131072]{1,0:T(4,128)}, bf16[64,16]{0,1:T(8,128)(2,1)S(1)}, /*index=5*/s32[]{:T(128)}, f32[]{:T(128)}, s32[]{:T(128)}) while((s32[]{:T(128)}, f32[65536]{0:T(1024)}, f32[3,65536]{1,0:T(4,128)}, s32[4,131072]{1,0:T(4,128)}, ...), condition=%wide.region_5.6_spmd.clone, body=%wide.region_0.5_spmd.clone.sunk | while | flops 293994496 | bytes 31983784 | solution.py:43
  4.2 3.4 %and_select_fusion.4 = (s32[1,131072]{1,0:T(1,128)S(1)}, s32[1,131072]{1,0:T(1,128)S(1)}) fusion(s32[4,131072]{1,0:T(4,128)} %get-tuple-element.181, s32[]{:T(128)} %get-tuple-element.170), kind=kLoop, calls=%fused_computation.5.clone.1 | loop fusion | flops 1441792 | bytes 1572868 | tf_op jit(solution)/shard_map/while/body/eval_jaxpr/jit(remainder)/select_n | solution.py:13
  7.6 3.8 %and_select_fusion.5 = s32[1,131072]{1,0:T(1,128)S(1)} fusion(s32[1,131072]{1,0:T(1,128)S(1)} %get-tuple-element.158, s32[4,131072]{1,0:T(4,128)} %get-tuple-element.181, s32[]{:T(128)} %get-tuple-element.170), kind=kLoop, calls=%fused_computation.6.clone.1 | loop fusion | flops 1572864 | bytes 1572868 | tf_op jit(solution)/shard_map/while/body/eval_jaxpr/jit(floor_divide)/jit(_where)/select_n | solution.py:14
  12.5 11.0 %select_reduce_fusion.2 = f32[4,131072]{1,0:T(4,128)S(1)} fusion(pred[16,131072]{1,0:T(8,128)(4,1)S(1)} %iota_compare_fusion.4, bf16[64,16]{0,1:T(8,128)(2,1)S(1)} %get-tuple-element.182, s32[131072]{0:T(1024)S(1)} %bitcast.553), kind=kOutput, calls=%fused_computation.clone.1 | convolution fusion | flops 286785536 | bytes 4720640 | tf_op jit(solution)/shard_map/while/body/eval_jaxpr/dot_general | solution.py:18
  30.3 2.9 %slice.38 = f32[3,2,65536]{2,1,0:T(2,128)} reshape(f32[3,131072]{1,0:T(4,128)S(1)} %bitcast.551) | data formatting | bytes 3145728 | tf_op jit(solution)/shard_map/while/body/eval_jaxpr/slice | solution.py:39
  33.1 3.9 %multiply_reduce_fusion.2 = f32[3,65536]{1,0:T(4,128)S(1)} fusion(f32[3,2,65536]{2,1,0:T(2,128)} %slice.38, f32[2,65536]{1,0:T(2,128)S(1)} %exponential_multiply_fusion.2), kind=kLoop, calls=%fused_computation.7.clone.1 | loop fusion | flops 589824 | bytes 2883584 | tf_op jit(solution)/shard_map/while/body/eval_jaxpr/reduce_sum | solution.py:39
  38.6 3.4 %and_select_fusion.4 = (s32[1,131072]{1,0:T(1,128)S(1)}, s32[1,131072]{1,0:T(1,128)S(1)}) fusion(s32[4,131072]{1,0:T(4,128)} %get-tuple-element.181, s32[]{:T(128)} %get-tuple-element.170), kind=kLoop, calls=%fused_computation.5.clone.1 | loop fusion | flops 1441792 | bytes 1572868 | tf_op jit(solution)/shard_map/while/body/eval_jaxpr/jit(remainder)/select_n | solution.py:13
  41.9 3.8 %and_select_fusion.5 = s32[1,131072]{1,0:T(1,128)S(1)} fusion(s32[1,131072]{1,0:T(1,128)S(1)} %get-tuple-element.158, s32[4,131072]{1,0:T(4,128)} %get-tuple-element.181, s32[]{:T(128)} %get-tuple-element.170), kind=kLoop, calls=%fused_computation.6.clone.1 | loop fusion | flops 1572864 | bytes 1572868 | tf_op jit(solution)/shard_map/while/body/eval_jaxpr/jit(floor_divide)/jit(_where)/select_n | solution.py:14
  46.8 11.0 %select_reduce_fusion.2 = f32[4,131072]{1,0:T(4,128)S(1)} fusion(pred[16,131072]{1,0:T(8,128)(4,1)S(1)} %iota_compare_fusion.4, bf16[64,16]{0,1:T(8,128)(2,1)S(1)} %get-tuple-element.182, s32[131072]{0:T(1024)S(1)} %bitcast.553), kind=kOutput, calls=%fused_computation.clone.1 | convolution fusion | flops 286785536 | bytes 4720640 | tf_op jit(solution)/shard_map/while/body/eval_jaxpr/dot_general | solution.py:18
  65.6 2.9 %slice.38 = f32[3,2,65536]{2,1,0:T(2,128)} reshape(f32[3,131072]{1,0:T(4,128)S(1)} %bitcast.551) | data formatting | bytes 3145728 | tf_op jit(solution)/shard_map/while/body/eval_jaxpr/slice | solution.py:39
  68.4 3.9 %multiply_reduce_fusion.2 = f32[3,65536]{1,0:T(4,128)S(1)} fusion(f32[3,2,65536]{2,1,0:T(2,128)} %slice.38, f32[2,65536]{1,0:T(2,128)S(1)} %exponential_multiply_fusion.2), kind=kLoop, calls=%fused_computation.7.clone.1 | loop fusion | flops 589824 | bytes 2883584 | tf_op jit(solution)/shard_map/while/body/eval_jaxpr/reduce_sum | solution.py:39
  73.9 3.4 %and_select_fusion.4 = (s32[1,131072]{1,0:T(1,128)S(1)}, s32[1,131072]{1,0:T(1,128)S(1)}) fusion(s32[4,131072]{1,0:T(4,128)} %get-tuple-element.181, s32[]{:T(128)} %get-tuple-element.170), kind=kLoop, calls=%fused_computation.5.clone.1 | loop fusion | flops 1441792 | bytes 1572868 | tf_op jit(solution)/shard_map/while/body/eval_jaxpr/jit(remainder)/select_n | solution.py:13
  77.2 3.8 %and_select_fusion.5 = s32[1,131072]{1,0:T(1,128)S(1)} fusion(s32[1,131072]{1,0:T(1,128)S(1)} %get-tuple-element.158, s32[4,131072]{1,0:T(4,128)} %get-tuple-element.181, s32[]{:T(128)} %get-tuple-element.170), kind=kLoop, calls=%fused_computation.6.clone.1 | loop fusion | flops 1572864 | bytes 1572868 | tf_op jit(solution)/shard_map/while/body/eval_jaxpr/jit(floor_divide)/jit(_where)/select_n | solution.py:14
  82.1 11.0 %select_reduce_fusion.2 = f32[4,131072]{1,0:T(4,128)S(1)} fusion(pred[16,131072]{1,0:T(8,128)(4,1)S(1)} %iota_compare_fusion.4, bf16[64,16]{0,1:T(8,128)(2,1)S(1)} %get-tuple-element.182, s32[131072]{0:T(1024)S(1)} %bitcast.553), kind=kOutput, calls=%fused_computation.clone.1 | convolution fusion | flops 286785536 | bytes 4720640 | tf_op jit(solution)/shard_map/while/body/eval_jaxpr/dot_general | solution.py:18
  100.8 2.9 %slice.38 = f32[3,2,65536]{2,1,0:T(2,128)} reshape(f32[3,131072]{1,0:T(4,128)S(1)} %bitcast.551) | data formatting | bytes 3145728 | tf_op jit(solution)/shard_map/while/body/eval_jaxpr/slice | solution.py:39
  103.7 3.9 %multiply_reduce_fusion.2 = f32[3,65536]{1,0:T(4,128)S(1)} fusion(f32[3,2,65536]{2,1,0:T(2,128)} %slice.38, f32[2,65536]{1,0:T(2,128)S(1)} %exponential_multiply_fusion.2), kind=kLoop, calls=%fused_computation.7.clone.1 | loop fusion | flops 589824 | bytes 2883584 | tf_op jit(solution)/shard_map/while/body/eval_jaxpr/reduce_sum | solution.py:39
  109.1 3.4 %and_select_fusion.4 = (s32[1,131072]{1,0:T(1,128)S(1)}, s32[1,131072]{1,0:T(1,128)S(1)}) fusion(s32[4,131072]{1,0:T(4,128)} %get-tuple-element.181, s32[]{:T(128)} %get-tuple-element.170), kind=kLoop, calls=%fused_computation.5.clone.1 | loop fusion | flops 1441792 | bytes 1572868 | tf_op jit(solution)/shard_map/while/body/eval_jaxpr/jit(remainder)/select_n | solution.py:13
  112.5 3.8 %and_select_fusion.5 = s32[1,131072]{1,0:T(1,128)S(1)} fusion(s32[1,131072]{1,0:T(1,128)S(1)} %get-tuple-element.158, s32[4,131072]{1,0:T(4,128)} %get-tuple-element.181, s32[]{:T(128)} %get-tuple-element.170), kind=kLoop, calls=%fused_computation.6.clone.1 | loop fusion | flops 1572864 | bytes 1572868 | tf_op jit(solution)/shard_map/while/body/eval_jaxpr/jit(floor_divide)/jit(_where)/select_n | solution.py:14
  117.4 11.0 %select_reduce_fusion.2 = f32[4,131072]{1,0:T(4,128)S(1)} fusion(pred[16,131072]{1,0:T(8,128)(4,1)S(1)} %iota_compare_fusion.4, bf16[64,16]{0,1:T(8,128)(2,1)S(1)} %get-tuple-element.182, s32[131072]{0:T(1024)S(1)} %bitcast.553), kind=kOutput, calls=%fused_computation.clone.1 | convolution fusion | flops 286785536 | bytes 4720640 | tf_op jit(solution)/shard_map/while/body/eval_jaxpr/dot_general | solution.py:18
  136.1 2.9 %slice.38 = f32[3,2,65536]{2,1,0:T(2,128)} reshape(f32[3,131072]{1,0:T(4,128)S(1)} %bitcast.551) | data formatting | bytes 3145728 | tf_op jit(solution)/shard_map/while/body/eval_jaxpr/slice | solution.py:39
  139.0 3.9 %multiply_reduce_fusion.2 = f32[3,65536]{1,0:T(4,128)S(1)} fusion(f32[3,2,65536]{2,1,0:T(2,128)} %slice.38, f32[2,65536]{1,0:T(2,128)S(1)} %exponential_multiply_fusion.2), kind=kLoop, calls=%fused_computation.7.clone.1 | loop fusion | flops 589824 | bytes 2883584 | tf_op jit(solution)/shard_map/while/body/eval_jaxpr/reduce_sum | solution.py:39
  223.5 11.5 %all-to-all-start = ((f32[128,1,4,2,256]{4,3,2,1,0:T(2,128)}), f32[128,1,4,2,256]{4,3,2,1,0:T(2,128)S(1)}, u32[]{:S(2)}, u32[]{:S(2)}) async-start(f32[128,1,4,2,256]{4,3,2,1,0:T(2,128)} %constant_dynamic-update-slice_fusion.1), calls=%async_computation | async-start | bytes 2097152 | tf_op jit(solution)/shard_map/all_to_all | solution.py:70
  235.1 18.9 %all-to-all-done = f32[128,1,4,2,256]{4,3,2,1,0:T(2,128)S(1)} async-done(((f32[128,1,4,2,256]{4,3,2,1,0:T(2,128)}), f32[128,1,4,2,256]{4,3,2,1,0:T(2,128)S(1)}, u32[]{:S(2)}, u32[]{:S(2)}) %all-to-all-start) | async-done | bytes 1048608 | tf_op jit(solution)/shard_map/all_to_all | solution.py:70
  (203 shorter events, 122.0 us)
Async XLA Ops:
  0.0 4.0 %copy-start.4 = (bf16[256]{0:T(256)(128)(2,1)S(1)}, bf16[256]{0:T(256)(128)(2,1)}, u32[]{:S(2)}) copy-start(bf16[256]{0:T(256)(128)(2,1)} %param.8) | copy-start | bytes 1540
  0.0 4.0 %copy-start.3 = (bf16[3,256]{1,0:T(4,128)(2,1)S(1)}, bf16[3,256]{1,0:T(4,128)(2,1)}, u32[]{:S(2)}) copy-start(bf16[3,256]{1,0:T(4,128)(2,1)} %param.7) | copy-start | bytes 4612
  33.1 3.9 %copy-start = (f32[3,65536]{1,0:T(4,128)S(1)}, f32[3,65536]{1,0:T(4,128)}, u32[]{:S(2)}) copy-start(f32[3,65536]{1,0:T(4,128)} %get-tuple-element.172) | copy-start | bytes 2359300 | tf_op jit(solution)/shard_map/while
  37.6 1.0 copy-start.1
  68.4 3.9 %copy-start = (f32[3,65536]{1,0:T(4,128)S(1)}, f32[3,65536]{1,0:T(4,128)}, u32[]{:S(2)}) copy-start(f32[3,65536]{1,0:T(4,128)} %get-tuple-element.172) | copy-start | bytes 2359300 | tf_op jit(solution)/shard_map/while
  72.9 1.0 copy-start.1
  103.7 3.9 %copy-start = (f32[3,65536]{1,0:T(4,128)S(1)}, f32[3,65536]{1,0:T(4,128)}, u32[]{:S(2)}) copy-start(f32[3,65536]{1,0:T(4,128)} %get-tuple-element.172) | copy-start | bytes 2359300 | tf_op jit(solution)/shard_map/while
  108.2 1.0 copy-start.1
  139.0 3.9 %copy-start = (f32[3,65536]{1,0:T(4,128)S(1)}, f32[3,65536]{1,0:T(4,128)}, u32[]{:S(2)}) copy-start(f32[3,65536]{1,0:T(4,128)} %get-tuple-element.172) | copy-start | bytes 2359300 | tf_op jit(solution)/shard_map/while
  143.5 1.0 copy-start.1
  146.9 88.1 %copy-start.2 = (s32[16,8]{0,1:T(8,128)S(1)}, s32[16,8]{0,1:T(8,128)}, u32[]{:S(2)}) copy-start(s32[16,8]{0,1:T(8,128)} %param.9) | copy-start | bytes 1540
  223.5 30.5 %all-to-all-start = ((f32[128,1,4,2,256]{4,3,2,1,0:T(2,128)}), f32[128,1,4,2,256]{4,3,2,1,0:T(2,128)S(1)}, u32[]{:S(2)}, u32[]{:S(2)}) async-start(f32[128,1,4,2,256]{4,3,2,1,0:T(2,128)} %constant_dynamic-update-slice_fusion.1), calls=%async_computation | async-start | bytes 2097152 | tf_op jit(solution)/shard_map/all_to_all | solution.py:70
